TPU v7x, 32 devices: a whole 2x2x4 slice. The times are simulated.
32 devices in a mesh: member: 8 (over y, x, core), lat: 4 (over z).
Axes of the slice: x: 2, y: 2, z: 4, core: 2. Of those that a mesh axis runs over, the one named last changes fastest.
Arguments:
- ensemble: float32 [16, 3, 1, 32, 1440], P('member', None, None, 'lat'), may hold values from -6 to 6
- observation: float32 [3, 1, 32, 1440], P(None, None, 'lat'), may hold values from -6 to 6
- valid_mask: int32 [16], P('member'), may hold values from 0 to 1, as said below
- band_start: int32 [4], P('lat'), may hold values from 0 to 713
Outputs:
- crps_field: float32 [3, 1, 32, 1440], P(None, None, ('lat', 'member'))
- score_table: float32 [3, 1], replicated
Inputs may be any that keep to these rules, and one draw needn't show every extreme that they name: `valid_mask`: exactly 13 entries are 1, at positions drawn afresh.
All inputs are finite; a program needn't handle non-finite values.
Results may differ from a plain program's by a relative error of at most 0.0001.
Values sent between devices are 32-bit elements; how exact they have to be, the bound alone decides.
A program may use at most 64 MiB of HBM per device.

v0:
```python
import math

import jax
import jax.numpy as jnp
from jax import lax
from jax.sharding import PartitionSpec as P

GRID_LAT = 721
GRID_LON = 1440


def on_device(ensemble, observation, valid_mask, band_start):
    member_flags = valid_mask.astype(jnp.float32)
    lat_rows = ensemble.shape[3]
    block_rows = lat_rows // lax.axis_size("member")
    row_offset = lax.axis_index("member") * block_rows
    members = lax.all_to_all(ensemble, "member", split_axis=3, concat_axis=0, tiled=True)
    all_flags = lax.all_gather(member_flags, "member", axis=0, tiled=True)
    slot_total = members.shape[0]
    truth_slice = lax.dynamic_slice_in_dim(observation, row_offset, block_rows, 2)
    valid_count = jnp.sum(all_flags)
    flag_column = all_flags[:, None, None, None, None]
    skill_term = jnp.sum(flag_column * jnp.abs(members - truth_slice[None]), axis=0)
    group_count = slot_total // 8
    blocks = members.reshape((group_count, 8) + members.shape[1:])
    block_flags = all_flags.reshape(group_count, 8)

    def block_sum(block_item):
        block_slab, flags_here = block_item

        def add_one(position, running_sum):
            one_slab = lax.dynamic_index_in_dim(block_slab, position, 0, keepdims=True)
            one_flag = lax.dynamic_index_in_dim(flags_here, position, 0, keepdims=False)
            return running_sum + one_flag * jnp.sum(
                flag_column * jnp.abs(one_slab - members), axis=0
            )

        return lax.fori_loop(0, 8, add_one, jnp.zeros(truth_slice.shape, jnp.float32))

    spread = jnp.sum(lax.map(block_sum, (blocks, block_flags)), axis=0)
    crps_field = skill_term / valid_count - spread / (2.0 * valid_count * (valid_count - 1.0))
    row_index = (band_start[0] + row_offset + jnp.arange(block_rows, dtype=jnp.int32)).astype(
        jnp.float32
    )
    weight = jnp.cos((90.0 - row_index * 180.0 / (GRID_LAT - 1)) * math.pi / 180.0)
    partial_sums = jnp.sum(crps_field * weight[:, None], axis=(2, 3))
    totals = lax.psum(partial_sums, ("member", "lat"))
    score_table = totals / (lax.axis_size("lat") * lat_rows * GRID_LON)
    return (crps_field, score_table)


def solution(mesh):
    placed = (
        P("member", None, None, "lat", None),
        P(None, None, "lat", None),
        P("member"),
        P("lat"),
    )
    return jax.shard_map(
        on_device,
        mesh=mesh,
        in_specs=placed,
        out_specs=(P(None, None, ("lat", "member"), None), P()),
        check_vma=False,
    )
```

profile of v0, /device:TPU:0, one launch (start us, length us, event | category | flops | bytes accessed | tf_op | source)
XLA Modules:
  0.0 100.7 jit_solution(13239071511892019307)
XLA Ops:
  0.6 1.9 %copy.26 = f32[2,3,1,8,1440]{4,1,2,0,3:T(4,128)} copy(f32[2,3,1,8,1440]{4,3,2,1,0:T(8,128)} %param.8) | data formatting | bytes 552960 | tf_op args[0]
  2.6 5.2 %all-to-all-start = ((f32[2,3,1,8,1440]{4,1,2,0,3:T(4,128)}), f32[2,3,1,8,1440]{4,1,2,0,3:T(4,128)S(1)}, u32[]{:S(2)}, u32[]{:S(2)}) async-start(f32[2,3,1,8,1440]{4,1,2,0,3:T(4,128)} %copy.26), calls=%async_computation | async-start | bytes 786432 | tf_op jit(solution)/shard_map/all_to_all | solution.py:17
  10.4 14.4 %all-reduce = f32[16]{0:T(128)S(1)} all-reduce(f32[16]{0:T(128)S(1)} %convert_dynamic-update-slice_fusion), channel_id=1, replica_groups=mesh['member'=8,'lat'=4] {'member'}, use_global_device_ids=true, to_apply=%add | all-reduce | flops 16 | bytes 128
  28.3 31.1 %while.25 = (s32[]{:T(128)}, f32[2,3,1,1,1440]{4,3,2,1,0:T(1,128)S(1)}, f32[2,8,3,1,1,1440]{5,4,3,2,1,0:T(1,128)S(1)}, f32[2,8]{1,0:T(2,128)S(1)}, f32[16,1,1,1,...) while((s32[]{:T(128)}, ...), condition=%wide.region_6.7_spmd, body=%wide.region_2.6_spmd.sunk | while | flops 285125 | bytes 780332 | solution.py:40
  28.4 15.4 %while.26 = (s32[]{:T(128)}, f32[3,1,1,1440]{3,2,1,0:T(1,128)S(1)}, f32[8]{0:T(128)S(1)}, f32[16,1,1,1,1]{0,4,3,2,1:T(1,128)S(1)}, f32[8,3,1,1,1440]{4,3,2,1,0:T...) while((s32[]{:T(128)}, f32[3,1,1,1440]{3,2,1,0:T(1,128)S(1)}, ...), condition=%wide.region_5.5_spmd.clone, body=%wide.region_3.4_spmd.clone.sunk | while | flops 285123 | bytes 466739 | solution.py:38
  29.6 0.7 broadcast_multiply_fusion.3
  31.5 0.7 broadcast_multiply_fusion.3
  33.4 0.7 broadcast_multiply_fusion.3
  35.4 0.7 broadcast_multiply_fusion.3
  37.3 0.7 broadcast_multiply_fusion.3
  39.2 0.7 broadcast_multiply_fusion.3
  41.2 0.7 broadcast_multiply_fusion.3
  43.1 0.7 broadcast_multiply_fusion.3
  43.9 15.4 %while.26 = (s32[]{:T(128)}, f32[3,1,1,1440]{3,2,1,0:T(1,128)S(1)}, f32[8]{0:T(128)S(1)}, f32[16,1,1,1,1]{0,4,3,2,1:T(1,128)S(1)}, f32[8,3,1,1,1440]{4,3,2,1,0:T...) while((s32[]{:T(128)}, f32[3,1,1,1440]{3,2,1,0:T(1,128)S(1)}, ...), condition=%wide.region_5.5_spmd.clone, body=%wide.region_3.4_spmd.clone.sunk | while | flops 285123 | bytes 466739 | solution.py:38
  45.1 0.7 broadcast_multiply_fusion.3
  47.0 0.7 broadcast_multiply_fusion.3
  49.0 0.7 broadcast_multiply_fusion.3
  50.9 0.7 broadcast_multiply_fusion.3
  52.8 0.7 broadcast_multiply_fusion.3
  54.8 0.7 broadcast_multiply_fusion.3
  56.7 0.7 broadcast_multiply_fusion.3
  58.6 0.7 broadcast_multiply_fusion.3
  59.5 0.8 multiply_reduce_fusion.2
  60.8 39.4 %psum.7 = f32[3,1]{0,1:T(1,128)S(1)} all-reduce(f32[3,1]{0,1:T(1,128)S(1)} %bitcast.50), channel_id=1, replica_groups=mesh['member'=8,'lat'=4] {'member','lat'}, use_global_device_ids=true, to_apply=%region_9.10 | all-reduce | flops 3 | bytes 24 | tf_op jit(solution)/shard_map/psum | solution.py:47
  (110 shorter events, 23.9 us)
Async XLA Ops:
  0.6 25.0 %copy-start = (f32[3,1,8,1440]{3,2,1,0:T(8,128)S(1)}, f32[3,1,8,1440]{3,2,1,0:T(8,128)}, u32[]{:S(2)}) copy-start(f32[3,1,8,1440]{3,2,1,0:T(8,128)} %param.9) | copy-start | bytes 414724
  2.6 25.2 %all-to-all-start = ((f32[2,3,1,8,1440]{4,1,2,0,3:T(4,128)}), f32[2,3,1,8,1440]{4,1,2,0,3:T(4,128)S(1)}, u32[]{:S(2)}, u32[]{:S(2)}) async-start(f32[2,3,1,8,1440]{4,1,2,0,3:T(4,128)} %copy.26), calls=%async_computation | async-start | bytes 786432 | tf_op jit(solution)/shard_map/all_to_all | solution.py:17
  7.8 0.7 copy-start.2
  9.7 0.7 copy-start.1
where the time goes:
time: 101 us
  blocking collectives  53.8 us (53%)
  other arithmetic  21.6 us (21%)
  local copies, waits for them, and re-layouts  16.1 us (16%)
  starting transfers between devices  5.2 us (5%)
  between operations  3.34 us (3%)
    psum x1, blocking collectives, on_device(): totals = lax.psum(partial_sums, ('member', 'lat'))  39.4 us
    unnamed x1, blocking collectives  14.4 us
    mul x16, other arithmetic, add_one(): one_flag * jnp.sum(flag_column * jnp.abs(one_slab - members), axis=0)  11.1 us
    dynamic_slice x16, local copies, waits for them, and re-layouts, add_one(): one_flag = lax.dynamic_index_in_dim(flags_here, position, 0, keepdims=False)  10.7 us
    reduce_sum x16, other arithmetic, add_one(): jnp.sum(flag_column * jnp.abs(one_slab - members), axis=0)  7.4 us
    all_to_all x1, starting transfers between devices, on_device(): lax.all_to_all(ensemble, 'member', split_axis=3, concat_axis=0, tiled=True)  5.2 us
    unnamed x10, local copies, waits for them, and re-layouts  3.83 us
  transfers between devices with their start and end apart: 1, of which 0 were waited for; matrix products, arithmetic and copies ran while one was open for 2% of the time, Pallas kernels for 0%

commit v1 on v0

v1 whole, which is shorter than its diff:
```python
import functools
import math

import jax
import jax.numpy as jnp
from jax import lax
from jax.experimental import pallas as pl
from jax.experimental.pallas import tpu as pltpu
from jax.sharding import PartitionSpec as P

GRID_LAT = 721
GRID_LON = 1440
LANES = 128
SUBLANES = 8
FILL = 1e30
MESH = pl.DeviceIdType.MESH


def round_up(value, step):
    return (value + step - 1) // step * step


def sort_pairs(count):
    pairs = []
    p = 1
    while p < count:
        k = p
        while k >= 1:
            for j in range(k % p, count - k, 2 * k):
                for i in range(min(k, count - j - k)):
                    if (i + j) // (2 * p) == (i + j + k) // (2 * p):
                        pairs.append((i + j, i + j + k))
            k //= 2
        p *= 2
    return pairs


def other(me, k, n):
    partner, bit = 0, 1
    while bit < n:
        here = (me // bit) % 2
        partner = partner + bit * (1 - here if k & bit else here)
        bit *= 2
    return partner


def chunk_of(ref, index, low, lon):
    wide = min(LANES, lon - low)
    value = ref[index + (pl.ds(low, wide),)]
    if wide < LANES:
        value = jnp.concatenate([value, jnp.zeros((SUBLANES, LANES - wide), value.dtype)], axis=1)
    return value


def kernel(
    n, nz, ens_ref, obs_ref, mask_ref, band_ref, field_ref, table_ref,
    ens_v, obs_v, packet, obs_rows, gathered, field_v, partials,
    load_sem, send_sem, recv_sem, psend_sem, precv_sem,
):
    held, variables, leads, rows, lon = ens_ref.shape
    units = variables * leads
    chunks = round_up(lon, LANES) // LANES
    lines = units * chunks
    group = round_up(lines + 1, SUBLANES)
    pitch = packet.shape[0] // n
    slots = n * held
    total = n * nz
    me = lax.axis_index("member")
    band = lax.axis_index("lat")
    mine = band * n + me

    loads = [
        pltpu.make_async_copy(ens_ref.at[m], ens_v.at[m], load_sem.at[m]) for m in range(held)
    ]
    loads.append(pltpu.make_async_copy(obs_ref, obs_v, load_sem.at[held]))
    for load in loads:
        load.start()

    barrier = pltpu.get_barrier_semaphore()
    for k in range(1, total):
        far = lax.rem(mine + k, total)
        pl.semaphore_signal(
            barrier, inc=1, device_id={"member": far % n, "lat": far // n}, device_id_type=MESH
        )

    for m in range(held):
        loads[m].wait()
        flag = jnp.full((SUBLANES, LANES), mask_ref[m], jnp.int32)
        keep = flag != 0
        for block in range(0, rows, SUBLANES):
            base = block * pitch + m * group
            for v in range(variables):
                for t in range(leads):
                    for c in range(chunks):
                        value = chunk_of(ens_v, (m, v, t, pl.ds(block, SUBLANES)), c * LANES, lon)
                        line = (v * leads + t) * chunks + c
                        packet[pl.ds(base + line, SUBLANES, stride=pitch), :] = jnp.where(
                            keep, value, FILL
                        )
            for line in range(lines, group):
                packet[pl.ds(base + line, SUBLANES, stride=pitch), :] = flag.astype(jnp.float32)

    pl.semaphore_wait(barrier, total - 1)

    sends = []
    for k in sorted(range(1, n), key=lambda k: (-bin(k // 2).count("1"), k)):
        far = other(me, k, n)
        sends.append(
            pltpu.make_async_remote_copy(
                src_ref=packet.at[pl.ds(pl.multiple_of(far * pitch, SUBLANES), held * group)],
                dst_ref=gathered.at[
                    pl.ds(pl.multiple_of(me * held * group, SUBLANES), held * group)
                ],
                send_sem=send_sem.at[k],
                recv_sem=recv_sem.at[k],
                device_id={"member": far, "lat": band},
                device_id_type=MESH,
            )
        )
        sends[-1].start()

    loads[held].wait()
    for block in range(0, rows, SUBLANES):
        for v in range(variables):
            for t in range(leads):
                for c in range(chunks):
                    line = (v * leads + t) * chunks + c
                    obs_rows[pl.ds(block * group + line, SUBLANES, stride=group), :] = chunk_of(
                        obs_v, (v, t, pl.ds(block, SUBLANES)), c * LANES, lon
                    )
    gathered[pl.ds(pl.multiple_of(me * held * group, SUBLANES), held * group), :] = packet[
        pl.ds(pl.multiple_of(me * pitch, SUBLANES), held * group), :
    ]
    row_number = jnp.full((1, LANES), band_ref[0] + me, jnp.int32).astype(jnp.float32)
    weight = jnp.cos((90.0 - row_number * 180.0 / (GRID_LAT - 1)) * math.pi / 180.0)

    for send in sends:
        send.wait_recv()

    flags = jnp.concatenate(
        [gathered[pl.ds(s * group + lines, 1), :] for s in range(slots)], axis=0
    )
    count = jnp.broadcast_to(jnp.sum(flags, axis=0, keepdims=True), (SUBLANES, LANES))
    per_one = 1.0 / count
    per_pair = per_one / (count - 1.0)
    skill_weight, spread_weight = [], []
    for i in range(slots):
        counted = i < count
        skill_weight.append(jnp.where(counted, per_one, 0.0))
        spread_weight.append(jnp.where(counted, (2.0 * i + 1.0 - count) * per_pair, 0.0))

    network = sort_pairs(slots)
    sums = [None] * units
    blocks = []
    for j in range(0, group, SUBLANES):
        x = [gathered[pl.ds(s * group + j, SUBLANES), :] for s in range(slots)]
        for a, b in network:
            x[a], x[b] = jnp.minimum(x[a], x[b]), jnp.maximum(x[a], x[b])
        truth = obs_rows[pl.ds(pl.multiple_of(me * group + j, SUBLANES), SUBLANES), :]
        score = None
        for i in range(slots):
            term = skill_weight[i] * jnp.abs(x[i] - truth) - spread_weight[i] * x[i]
            score = term if score is None else score + term
        blocks.append(score)
        line = j + lax.broadcasted_iota(jnp.int32, (SUBLANES, LANES), 0)
        for u in range(units):
            low, high = u * chunks, (u + 1) * chunks
            if low < j + SUBLANES and j < high:
                part = jnp.where((line >= low) & (line < high), score, 0.0)
                sums[u] = part if sums[u] is None else sums[u] + part

    lane = lax.broadcasted_iota(jnp.int32, (1, LANES), 1)
    row = jnp.zeros((1, LANES), jnp.float32)
    for u in range(units):
        one = jnp.sum(jnp.sum(sums[u], axis=0, keepdims=True), axis=1, keepdims=True)
        row = jnp.where(lane == u, one, row)
    partials[pl.ds(mine, 1), :] = row * weight

    for send in sends:
        send.wait_send()
    for line in range(lines):
        u, c = line // chunks, line % chunks
        wide = min(LANES, lon - c * LANES)
        score = blocks[line // SUBLANES]
        at = line % SUBLANES
        field_v[u // leads, u % leads, :, pl.ds(c * LANES, wide)] = score[at : at + 1, :wide]
    out = pltpu.make_async_copy(field_v, field_ref, load_sem.at[0])
    out.start()

    shares = []
    for k in range(1, total):
        far = lax.rem(mine + k, total)
        shares.append(
            pltpu.make_async_remote_copy(
                src_ref=partials.at[pl.ds(mine, 1)],
                dst_ref=partials.at[pl.ds(mine, 1)],
                send_sem=psend_sem.at[k],
                recv_sem=precv_sem.at[k],
                device_id={"member": far % n, "lat": far // n},
                device_id_type=MESH,
            )
        )
        shares[-1].start()
    for share in shares:
        share.wait_recv()
    summed = jnp.sum(partials[...], axis=0, keepdims=True)
    spot = lax.broadcasted_iota(jnp.int32, (units, LANES), 0)
    across = lax.broadcasted_iota(jnp.int32, (units, LANES), 1)
    diagonal = jnp.where(spot == across, jnp.broadcast_to(summed, (units, LANES)), 0.0)
    table_ref[...] = jnp.sum(diagonal, axis=1, keepdims=True) / (nz * rows * GRID_LON)
    for share in shares:
        share.wait_send()
    out.wait()


def on_device(n, nz, ensemble, observation, valid_mask, band_start):
    held, variables, leads, rows, lon = ensemble.shape
    assert rows == n and rows % SUBLANES == 0
    units = variables * leads
    chunks = round_up(lon, LANES) // LANES
    group = round_up(units * chunks + 1, SUBLANES)
    pitch = held * group
    if pitch % 16 == 0:
        pitch += SUBLANES
    total = n * nz
    field, table = pl.pallas_call(
        functools.partial(kernel, n, nz),
        out_shape=(
            jax.ShapeDtypeStruct((variables, leads, rows // n, lon), jnp.float32),
            jax.ShapeDtypeStruct((units, 1), jnp.float32),
        ),
        in_specs=[
            pl.BlockSpec(memory_space=pl.ANY),
            pl.BlockSpec(memory_space=pl.ANY),
            pl.BlockSpec(memory_space=pltpu.SMEM),
            pl.BlockSpec(memory_space=pltpu.SMEM),
        ],
        out_specs=(
            pl.BlockSpec(memory_space=pl.ANY),
            pl.BlockSpec(memory_space=pltpu.VMEM),
        ),
        scratch_shapes=[
            pltpu.VMEM(ensemble.shape, jnp.float32),
            pltpu.VMEM(observation.shape, jnp.float32),
            pltpu.VMEM((n * pitch, LANES), jnp.float32),
            pltpu.VMEM((n * group, LANES), jnp.float32),
            pltpu.VMEM((n * held * group, LANES), jnp.float32),
            pltpu.VMEM((variables, leads, rows // n, lon), jnp.float32),
            pltpu.VMEM((total, LANES), jnp.float32),
            pltpu.SemaphoreType.DMA((held + 1,)),
            pltpu.SemaphoreType.DMA((n,)),
            pltpu.SemaphoreType.DMA((n,)),
            pltpu.SemaphoreType.DMA((total,)),
            pltpu.SemaphoreType.DMA((total,)),
        ],
        compiler_params=pltpu.CompilerParams(collective_id=0, has_side_effects=True),
        name="fair_crps",
    )(ensemble, observation, valid_mask, band_start)
    return field, table.reshape(variables, leads)


def solution(mesh):
    placed = (
        P("member", None, None, "lat", None),
        P(None, None, "lat", None),
        P("member"),
        P("lat"),
    )
    return jax.shard_map(
        functools.partial(on_device, mesh.shape["member"], mesh.shape["lat"]),
        mesh=mesh,
        in_specs=placed,
        out_specs=(P(None, None, ("lat", "member"), None), P()),
        check_vma=False,
    )
```

time: 101 us -> 21.9 us (0.22)
  blocking collectives: 53.8 us -> 0 us
  other arithmetic: 21.6 us -> 0 us
  Pallas kernels: 0 us -> 17.8 us
  local copies, waits for them, and re-layouts: 16.1 us -> 2.57 us
  starting transfers between devices: 5.2 us -> 0 us
  between operations: 3.34 us -> 1.29 us
    psum x1 -> x0, blocking collectives: 39.4 us -> none  [on_device(): totals = lax.psum(partial_sums, ('member', 'lat'))]
    pallas_call x0 -> x1, Pallas kernels: none -> 17.8 us  [on_device(): pl.pallas_call(functools.partial(kernel, n, nz), out_shape=(jax.ShapeDtyp...]
    unnamed x1 -> x0, blocking collectives: 14.4 us -> none
    mul x16 -> x0, other arithmetic: 11.1 us -> none  [add_one(): one_flag * jnp.sum(flag_column * jnp.abs(one_slab - members), axis=0)]
    dynamic_slice x33 -> x0, local copies, waits for them, and re-layouts: 10.9 us -> none  [the longest x16 10.7 us: add_one(): one_flag = lax.dynamic_index_in_dim(flags_here, position, 0, keepdims=False)]
    reduce_sum x20 -> x0, other arithmetic: 9.12 us -> none  [the longest x16 7.4 us: add_one(): jnp.sum(flag_column * jnp.abs(one_slab - members), axis=0)]
    all_to_all x1 -> x0, starting transfers between devices: 5.2 us -> none  [on_device(): lax.all_to_all(ensemble, 'member', split_axis=3, concat_axis=0, tiled=True)]
    unnamed x10 -> x3, local copies, waits for them, and re-layouts: 3.83 us -> 1.98 us
  transfers between devices with their start and end apart: 1 -> 0, of which waited for: 0 -> 0; matrix products, arithmetic and copies ran while one was open for 2% -> 0% of each run, Pallas kernels for 0% -> 0%
where the time goes in v1:
time: 21.9 us; the launch traced here: 21.7 us
  Pallas kernels  17.8 us (81%)
  local copies, waits for them, and re-layouts  2.57 us (12%)
  between operations  1.29 us (6%)
    pallas_call x1, Pallas kernels, on_device(): pl.pallas_call(functools.partial(kernel, n, nz), out_shape=(jax.ShapeDtyp...  17.8 us
    unnamed x3, local copies, waits for them, and re-layouts  1.98 us
    pallas_call x1, local copies, waits for them, and re-layouts, on_device(): pl.pallas_call(functools.partial(kernel, n, nz), out_shape=(jax.ShapeDtyp...  0.6 us

profile of v1, /device:TPU:0, one launch (start us, length us, event | category | flops | bytes accessed | tf_op | source)
XLA Modules:
  0.0 21.7 jit_solution(10790207203153825497)
XLA Ops:
  1.3 17.8 %fair_crps.1 = (f32[3,1,1,1440]{3,2,1,0:T(1,128)}, f32[3,1]{1,0:T(4,128)}) custom-call(f32[2,3,1,8,1440]{4,3,2,1,0:T(8,128)} %ens_ref.1, f32[3,1,8,1440]{3,2,1,0:T(8,128)} %obs_ref.1, s32[2]{0:T(128)} %mask_ref.1, s32[1]{0:T(128)S(6)} %copy.8.band_ref), custom_call_target="tpu_custom_call" | custom-call | tf_op jit(solution)/shard_map/fair_crps/pallas_call | solution.py:226
  19.1 0.0 copy-start
  19.1 0.6 %copy-done = f32[3,1]{1,0:T(4,128)S(1)} copy-done((f32[3,1]{1,0:T(4,128)S(1)}, f32[3,1]{1,0:T(4,128)}, u32[]{:S(2)}) %copy-start) | copy-done | bytes 36
  19.7 0.6 %copy.6 = f32[3,1]{0,1:T(1,128)} copy(f32[3,1]{1,0:T(4,128)S(1)} %copy-done) | data formatting | bytes 24 | tf_op jit(solution)/shard_map/fair_crps/pallas_call | solution.py:226
  20.3 1.3 %copy.9 = f32[3,1,1,1440]{3,2,1,0:T(1,128)} copy(f32[3,1,1,1440]{3,2,1,0:T(1,128)} %get-tuple-element.6) | data formatting | bytes 34560
Async XLA Ops:
  19.1 0.7 %copy-start = (f32[3,1]{1,0:T(4,128)S(1)}, f32[3,1]{1,0:T(4,128)}, u32[]{:S(2)}) copy-start(f32[3,1]{1,0:T(4,128)} %get-tuple-element.3) | copy-start | bytes 40

commit v2 on v1

v2 whole, which is shorter than its diff:
```python
import functools
import math

import jax
import jax.numpy as jnp
from jax import lax
from jax.experimental import pallas as pl
from jax.experimental.pallas import tpu as pltpu
from jax.sharding import PartitionSpec as P

GRID_LAT = 721
GRID_LON = 1440
LANES = 128
SUBLANES = 8
FILL = 1e30
VMEM_BYTES = 67_043_328 - 65_536
MESH = pl.DeviceIdType.MESH


def round_up(value, step):
    return (value + step - 1) // step * step


def sort_pairs(count):
    pairs = []
    p = 1
    while p < count:
        k = p
        while k >= 1:
            for j in range(k % p, count - k, 2 * k):
                for i in range(min(k, count - j - k)):
                    if (i + j) // (2 * p) == (i + j + k) // (2 * p):
                        pairs.append((i + j, i + j + k))
            k //= 2
        p *= 2
    return pairs


def other(me, k, n):
    partner, bit = 0, 1
    while bit < n:
        here = (me // bit) % 2
        partner = partner + bit * (1 - here if k & bit else here)
        bit *= 2
    return partner


class Packing:
    def __init__(self, units, lon):
        self.units, self.full, self.tail = units, lon // LANES, lon % LANES
        self.beside = LANES // self.tail if self.tail else 1
        self.tails = round_up(units, self.beside) // self.beside if self.tail else 0
        self.lines = units * self.full + self.tails

    def line(self, load, number):
        if number < self.units * self.full:
            return load(number // self.full, number % self.full * LANES, LANES)
        first = (number - self.units * self.full) * self.beside
        last = min(first + self.beside, self.units)
        parts = [load(u, self.full * LANES, self.tail) for u in range(first, last)]
        empty = LANES - self.tail * len(parts)
        if empty:
            parts.append(jnp.zeros((SUBLANES, empty), jnp.float32))
        return jnp.concatenate(parts, axis=1) if len(parts) > 1 else parts[0]

    def mask(self, unit, line, lane):
        inside = (line >= unit * self.full) & (line < (unit + 1) * self.full)
        if self.tail:
            low = unit % self.beside * self.tail
            at = self.units * self.full + unit // self.beside
            inside |= (line == at) & (lane >= low) & (lane < low + self.tail)
        return inside

    def pieces(self):
        for u in range(self.units):
            for c in range(self.full):
                yield u, c * LANES, LANES, u * self.full + c, 0
            if self.tail:
                at = self.units * self.full + u // self.beside
                yield u, self.full * LANES, self.tail, at, u % self.beside * self.tail


def kernel(
    n, nz, ens_ref, obs_ref, mask_ref, band_ref, field_ref, table_ref,
    ens_v, obs_v, mask_s, packet, obs_rows, gathered, partials,
    load_sem, send_sem, recv_sem, psend_sem, precv_sem, ready_sem,
):
    held, variables, leads, rows, lon = ens_ref.shape
    units = variables * leads
    packing = Packing(units, lon)
    lines = packing.lines
    pitch = packet.shape[0] // n
    stride = obs_rows.shape[0] // n
    slots = n * held
    total = n * nz
    me = lax.axis_index("member")
    band = lax.axis_index("lat")
    mine = band * n + me

    loads = [pltpu.make_async_copy(mask_ref, mask_s, load_sem.at[held + 1])]
    loads += [pltpu.make_async_copy(ens_ref.at[m], ens_v.at[m], load_sem.at[m]) for m in range(held)]
    loads.append(pltpu.make_async_copy(obs_ref, obs_v, load_sem.at[held]))
    for load in loads:
        load.start()

    plane = [{"member": other(me, k, n), "lat": band} for k in range(1, n)]
    line_peers = [{"member": me, "lat": lax.rem(band + k, nz)} for k in range(1, nz)]
    barrier = pltpu.get_barrier_semaphore()
    for peer in plane + line_peers:
        pl.semaphore_signal(barrier, inc=1, device_id=peer, device_id_type=MESH)

    loads[0].wait()
    for m in range(held):
        loads[1 + m].wait()
        flag = jnp.full((SUBLANES, LANES), mask_s[m], jnp.int32)
        keep = flag != 0
        for block in range(0, rows, SUBLANES):
            base = block * pitch

            def load(u, low, wide):
                return ens_v[m, u // leads, u % leads, pl.ds(block, SUBLANES), pl.ds(low, wide)]

            for line in range(lines):
                packet[pl.ds(base + m * lines + line, SUBLANES, stride=pitch), :] = jnp.where(
                    keep, packing.line(load, line), FILL
                )
            for line in range(held * lines + m, pitch, held):
                packet[pl.ds(base + line, SUBLANES, stride=pitch), :] = flag.astype(jnp.float32)

    pl.semaphore_wait(barrier, n - 1 + nz - 1)

    sends = []
    for k in sorted(range(1, n), key=lambda k: (-bin(k // 2).count("1"), k)):
        sends.append(
            pltpu.make_async_remote_copy(
                src_ref=packet.at[
                    pl.ds(pl.multiple_of(plane[k - 1]["member"] * pitch, SUBLANES), pitch)
                ],
                dst_ref=gathered.at[pl.ds(pl.multiple_of(me * pitch, SUBLANES), pitch)],
                send_sem=send_sem.at[k],
                recv_sem=recv_sem.at[k],
                device_id=plane[k - 1],
                device_id_type=MESH,
            )
        )
        sends[-1].start()
    for peer in line_peers:
        pl.semaphore_signal(ready_sem, inc=1, device_id=peer, device_id_type=MESH)

    loads[1 + held].wait()
    for block in range(0, rows, SUBLANES):

        def load(u, low, wide):
            return obs_v[u // leads, u % leads, pl.ds(block, SUBLANES), pl.ds(low, wide)]

        for line in range(lines):
            obs_rows[pl.ds(block * stride + line, SUBLANES, stride=stride), :] = packing.line(
                load, line
            )
    gathered[pl.ds(pl.multiple_of(me * pitch, SUBLANES), pitch), :] = packet[
        pl.ds(pl.multiple_of(me * pitch, SUBLANES), pitch), :
    ]
    row_number = jnp.full((1, LANES), band_ref[0] + me, jnp.int32).astype(jnp.float32)
    weight = jnp.cos((90.0 - row_number * 180.0 / (GRID_LAT - 1)) * math.pi / 180.0)
    pl.semaphore_wait(ready_sem, nz - 1)

    for send in sends:
        send.wait_recv()

    flags = jnp.concatenate(
        [gathered[pl.ds(d * pitch + held * lines, held), :] for d in range(n)], axis=0
    )
    count = jnp.broadcast_to(jnp.sum(flags, axis=0, keepdims=True), (SUBLANES, LANES))
    per_one = 1.0 / count
    per_pair = per_one / (count - 1.0)
    skill_weight, spread_weight = [], []
    for i in range(slots):
        counted = i < count
        skill_weight.append(jnp.where(counted, per_one, 0.0))
        spread_weight.append(jnp.where(counted, (2.0 * i + 1.0 - count) * per_pair, 0.0))

    network = sort_pairs(slots)
    sums = [None] * units
    blocks = []
    lane = lax.broadcasted_iota(jnp.int32, (SUBLANES, LANES), 1)
    for j in range(0, lines, SUBLANES):
        x = [
            gathered[pl.ds(s // held * pitch + s % held * lines + j, SUBLANES), :]
            for s in range(slots)
        ]
        for a, b in network:
            x[a], x[b] = jnp.minimum(x[a], x[b]), jnp.maximum(x[a], x[b])
        truth = obs_rows[pl.ds(pl.multiple_of(me * stride + j, SUBLANES), SUBLANES), :]
        score = None
        for i in range(slots):
            term = skill_weight[i] * jnp.abs(x[i] - truth) - spread_weight[i] * x[i]
            score = term if score is None else score + term
        blocks.append(score)
        line = j + lax.broadcasted_iota(jnp.int32, (SUBLANES, LANES), 0)
        for u in range(units):
            part = jnp.where(packing.mask(u, line, lane), score, 0.0)
            sums[u] = part if sums[u] is None else sums[u] + part

    lane = lax.broadcasted_iota(jnp.int32, (1, LANES), 1)
    row = jnp.zeros((1, LANES), jnp.float32)
    for u in range(units):
        one = jnp.sum(jnp.sum(sums[u], axis=0, keepdims=True), axis=1, keepdims=True)
        row = jnp.where(lane == u, one, row)
    partials[pl.ds(mine, 1), :] = row * weight

    for send in sends:
        send.wait_send()

    def share_with(far):
        return pltpu.make_async_remote_copy(
            src_ref=partials.at[pl.ds(mine, 1)],
            dst_ref=partials.at[pl.ds(mine, 1)],
            send_sem=psend_sem.at[far],
            recv_sem=precv_sem.at[mine],
            device_id={"member": far % n, "lat": far // n},
            device_id_type=MESH,
        )

    def share_from(far):
        return pltpu.make_async_remote_copy(
            src_ref=partials.at[pl.ds(mine, 1)],
            dst_ref=partials.at[pl.ds(far, 1)],
            send_sem=psend_sem.at[far],
            recv_sem=precv_sem.at[far],
            device_id={"member": far % n, "lat": far // n},
            device_id_type=MESH,
        )

    for far in range(total):
        pl.when(far != mine)(lambda far=far: share_with(far).start())

    for u, low, wide, at, first in packing.pieces():
        piece = blocks[at // SUBLANES][at % SUBLANES : at % SUBLANES + 1, first : first + wide]
        field_ref[u // leads, u % leads, :, pl.ds(low, wide)] = piece

    for far in range(total):
        pl.when(far != mine)(lambda far=far: share_from(far).wait_recv())
    summed = jnp.sum(partials[...], axis=0, keepdims=True)
    table_ref[...] = summed[:, :units] / (nz * rows * GRID_LON)
    for far in range(total):
        pl.when(far != mine)(lambda far=far: share_with(far).wait_send())


def on_device(n, nz, ensemble, observation, valid_mask, band_start):
    held, variables, leads, rows, lon = ensemble.shape
    assert rows == n and rows % SUBLANES == 0
    units = variables * leads
    packing = Packing(units, lon)
    pitch = round_up(held * packing.lines + held, SUBLANES)
    stride = round_up(packing.lines, SUBLANES)
    total = n * nz
    field, table = pl.pallas_call(
        functools.partial(kernel, n, nz),
        out_shape=(
            pltpu.VMEM((variables, leads, rows // n, lon), jnp.float32),
            pltpu.VMEM((1, units), jnp.float32),
        ),
        in_specs=[pl.BlockSpec(memory_space=pltpu.HBM)] * 3 + [pl.BlockSpec(memory_space=pltpu.SMEM)],
        out_specs=(
            pl.BlockSpec(memory_space=pltpu.VMEM),
            pl.BlockSpec(memory_space=pltpu.VMEM),
        ),
        scratch_shapes=[
            pltpu.VMEM(ensemble.shape, jnp.float32),
            pltpu.VMEM(observation.shape, jnp.float32),
            pltpu.SMEM(valid_mask.shape, jnp.int32),
            pltpu.VMEM((n * pitch, LANES), jnp.float32),
            pltpu.VMEM((n * stride, LANES), jnp.float32),
            pltpu.VMEM((n * pitch + SUBLANES, LANES), jnp.float32),
            pltpu.VMEM((total, LANES), jnp.float32),
            pltpu.SemaphoreType.DMA((held + 2,)),
            pltpu.SemaphoreType.DMA((n,)),
            pltpu.SemaphoreType.DMA((n,)),
            pltpu.SemaphoreType.DMA((total,)),
            pltpu.SemaphoreType.DMA((total,)),
            pltpu.SemaphoreType.REGULAR,
        ],
        compiler_params=pltpu.CompilerParams(
            collective_id=0, has_side_effects=True, vmem_limit_bytes=VMEM_BYTES
        ),
        name="fair_crps",
    )(ensemble, observation, valid_mask, band_start)
    return field, table.reshape(variables, leads)


def solution(mesh):
    placed = (
        P("member", None, None, "lat", None),
        P(None, None, "lat", None),
        P("member"),
        P("lat"),
    )
    return jax.shard_map(
        functools.partial(on_device, mesh.shape["member"], mesh.shape["lat"]),
        mesh=mesh,
        in_specs=placed,
        out_specs=(P(None, None, ("lat", "member"), None), P()),
        check_vma=False,
    )
```

time: 21.9 us -> 18.3 us (0.84)
  Pallas kernels: 17.8 us -> 15.8 us
  local copies, waits for them, and re-layouts: 2.57 us -> 1.12 us
    pallas_call x1, Pallas kernels: 17.8 us -> 15.8 us  [on_device(): pl.pallas_call(functools.partial(kernel, n, nz), out_shape=(pltpu.VMEM((v...]
    unnamed x3 -> x2, local copies, waits for them, and re-layouts: 1.98 us -> 1.12 us
    pallas_call x1 -> x0, local copies, waits for them, and re-layouts: 0.6 us -> none  [on_device(): pl.pallas_call(functools.partial(kernel, n, nz), out_shape=(jax.ShapeDtyp...]
where the time goes in v2:
time: 18.3 us; the launch traced here: 18.2 us
  Pallas kernels  15.8 us (86%)
  between operations  1.29 us (7%)
  local copies, waits for them, and re-layouts  1.12 us (6%)
    pallas_call x1, Pallas kernels, on_device(): pl.pallas_call(functools.partial(kernel, n, nz), out_shape=(pltpu.VMEM((v...  15.8 us
    unnamed x2, local copies, waits for them, and re-layouts  1.12 us

profile of v2, /device:TPU:0, one launch (start us, length us, event | category | flops | bytes accessed | tf_op | source)
XLA Modules:
  0.0 18.2 jit_solution(12596630830954175180)
XLA Ops:
  1.3 15.8 %fair_crps.1 = (f32[3,1,1,1440]{3,2,1,0:T(1,128)S(1)}, f32[1,3]{1,0:T(1,128)S(1)}) custom-call(f32[2,3,1,8,1440]{4,3,2,1,0:T(8,128)} %ens_ref.1, f32[3,1,8,1440]{3,2,1,0:T(8,128)} %obs_ref.1, s32[2]{0:T(128)} %mask_ref.1, s32[1]{0:T(128)S(6)} %copy.10.band_ref), custom_call_target="tpu_custom_call" | custom-call | tf_op jit(solution)/shard_map/fair_crps/pallas_call | solution.py:257
  17.1 0.6 %copy.8 = f32[3,1,1,1440]{3,2,1,0:T(1,128)} copy(f32[3,1,1,1440]{3,2,1,0:T(1,128)S(1)} %get-tuple-element.6) | data formatting | bytes 34560
  17.7 0.5 %copy.9 = f32[3,1]{0,1:T(1,128)} copy(f32[3,1]{0,1:T(1,128)S(1)} %bitcast.1) | data formatting | bytes 24

commit v3 on v2

--- a/solution.py
+++ b/solution.py
@@ -100,14 +100,13 @@
     loads = [pltpu.make_async_copy(mask_ref, mask_s, load_sem.at[held + 1])]
     loads += [pltpu.make_async_copy(ens_ref.at[m], ens_v.at[m], load_sem.at[m]) for m in range(held)]
     loads.append(pltpu.make_async_copy(obs_ref, obs_v, load_sem.at[held]))
-    for load in loads:
-        load.start()
-
     plane = [{"member": other(me, k, n), "lat": band} for k in range(1, n)]
     line_peers = [{"member": me, "lat": lax.rem(band + k, nz)} for k in range(1, nz)]
     barrier = pltpu.get_barrier_semaphore()
-    for peer in plane + line_peers:
+    for peer in plane[::-1] + line_peers:
         pl.semaphore_signal(barrier, inc=1, device_id=peer, device_id_type=MESH)
+    for load in loads:
+        load.start()
 
     loads[0].wait()
     for m in range(held):
@@ -244,6 +243,17 @@
     table_ref[...] = summed[:, :units] / (nz * rows * GRID_LON)
     for far in range(total):
         pl.when(far != mine)(lambda far=far: share_with(far).wait_send())
+
+
+def write_out(field_ref, table_ref, field_out, table_out, sem):
+    copies = [
+        pltpu.make_async_copy(field_ref, field_out, sem.at[0]),
+        pltpu.make_async_copy(table_ref, table_out, sem.at[1]),
+    ]
+    for copy in copies:
+        copy.start()
+    for copy in copies:
+        copy.wait()
 
 
 def on_device(n, nz, ensemble, observation, valid_mask, band_start):
@@ -285,6 +295,17 @@
         ),
         name="fair_crps",
     )(ensemble, observation, valid_mask, band_start)
+    field, table = pl.pallas_call(
+        write_out,
+        out_shape=(
+            jax.ShapeDtypeStruct(field.shape, jnp.float32),
+            jax.ShapeDtypeStruct(table.shape, jnp.float32),
+        ),
+        in_specs=[pl.BlockSpec(memory_space=pltpu.VMEM)] * 2,
+        out_specs=(pl.BlockSpec(memory_space=pltpu.HBM),) * 2,
+        scratch_shapes=[pltpu.SemaphoreType.DMA((2,))],
+        name="write_out",
+    )(*(pltpu.with_memory_space_constraint(a, pltpu.VMEM) for a in (field, table)))
     return field, table.reshape(variables, leads)
 
 

time: 18.3 us -> 17.8 us (0.973)
  local copies, waits for them, and re-layouts: 1.12 us -> 0 us
  Pallas kernels: 15.8 us -> 16.3 us
    unnamed x2 -> x0, local copies, waits for them, and re-layouts: 1.12 us -> none
    pallas_call x0 -> x1, Pallas kernels: none -> 0.63 us  [on_device(): pl.pallas_call(write_out, out_shape=(jax.ShapeDtypeStruct(field.shape, jn...]
where the time goes in v3:
time: 17.8 us; the launch traced here: 17.6 us
  Pallas kernels  16.3 us (92%)
  between operations  1.28 us (7%)
    pallas_call x1, Pallas kernels, on_device(): pl.pallas_call(functools.partial(kernel, n, nz), out_shape=(pltpu.VMEM((v...  15.7 us
    pallas_call x1, Pallas kernels, on_device(): pl.pallas_call(write_out, out_shape=(jax.ShapeDtypeStruct(field.shape, jn...  0.63 us

profile of v3, /device:TPU:0, one launch (start us, length us, event | category | flops | bytes accessed | tf_op | source)
XLA Modules:
  0.0 17.6 jit_solution(7444457798495993599)
XLA Ops:
  1.3 15.7 %fair_crps.1 = (f32[3,1,1,1440]{3,2,1,0:T(1,128)S(1)}, f32[1,3]{1,0:T(1,128)S(1)}) custom-call(f32[2,3,1,8,1440]{4,3,2,1,0:T(8,128)} %ens_ref.1, f32[3,1,8,1440]{3,2,1,0:T(8,128)} %obs_ref.1, s32[2]{0:T(128)} %mask_ref.1, s32[1]{0:T(128)S(6)} %copy.6.band_ref), custom_call_target="tpu_custom_call" | custom-call | tf_op jit(solution)/shard_map/fair_crps/pallas_call | solution.py:267
  17.0 0.6 %write_out.1 = (f32[3,1,1,1440]{3,2,1,0:T(1,128)}, f32[1,3]{1,0:T(1,128)}) custom-call(f32[3,1,1,1440]{3,2,1,0:T(1,128)S(1)} %get-tuple-element.6.field_ref, f32[1,3]{1,0:T(1,128)S(1)} %get-tuple-element.7.table_ref), custom_call_target="tpu_custom_call" | custom-call | tf_op jit(solution)/shard_map/write_out/pallas_call | solution.py:298

commit v4 on v3

--- a/solution.py
+++ b/solution.py
@@ -51,6 +51,7 @@
         self.beside = LANES // self.tail if self.tail else 1
         self.tails = round_up(units, self.beside) // self.beside if self.tail else 0
         self.lines = units * self.full + self.tails
+        self.used = (units - 1) % self.beside * self.tail + self.tail
 
     def line(self, load, number):
         if number < self.units * self.full:
@@ -109,6 +110,7 @@
         load.start()
 
     loads[0].wait()
+    free = lax.broadcasted_iota(jnp.int32, (SUBLANES, LANES), 1) >= packing.used
     for m in range(held):
         loads[1 + m].wait()
         flag = jnp.full((SUBLANES, LANES), mask_s[m], jnp.int32)
@@ -120,11 +122,12 @@
                 return ens_v[m, u // leads, u % leads, pl.ds(block, SUBLANES), pl.ds(low, wide)]
 
             for line in range(lines):
-                packet[pl.ds(base + m * lines + line, SUBLANES, stride=pitch), :] = jnp.where(
-                    keep, packing.line(load, line), FILL
-                )
+                value = jnp.where(keep, packing.line(load, line), FILL)
+                if line == lines - 1:
+                    value = jnp.where(free, flag.astype(jnp.float32), value)
+                packet[pl.ds(base + m * lines + line, SUBLANES, stride=pitch), :] = value
             for line in range(held * lines + m, pitch, held):
-                packet[pl.ds(base + line, SUBLANES, stride=pitch), :] = flag.astype(jnp.float32)
+                packet[pl.ds(base + line, SUBLANES, stride=pitch), :] = jnp.zeros_like(value)
 
     pl.semaphore_wait(barrier, n - 1 + nz - 1)
 
@@ -133,9 +136,11 @@
         sends.append(
             pltpu.make_async_remote_copy(
                 src_ref=packet.at[
-                    pl.ds(pl.multiple_of(plane[k - 1]["member"] * pitch, SUBLANES), pitch)
+                    pl.ds(pl.multiple_of(plane[k - 1]["member"] * pitch, SUBLANES), held * lines)
                 ],
-                dst_ref=gathered.at[pl.ds(pl.multiple_of(me * pitch, SUBLANES), pitch)],
+                dst_ref=gathered.at[
+                    pl.ds(pl.multiple_of(me * pitch, SUBLANES), held * lines)
+                ],
                 send_sem=send_sem.at[k],
                 recv_sem=recv_sem.at[k],
                 device_id=plane[k - 1],
@@ -167,9 +172,16 @@
         send.wait_recv()
 
     flags = jnp.concatenate(
-        [gathered[pl.ds(d * pitch + held * lines, held), :] for d in range(n)], axis=0
+        [
+            gathered[pl.ds(s // held * pitch + s % held * lines + lines - 1, 1), :]
+            for s in range(slots)
+        ],
+        axis=0,
     )
-    count = jnp.broadcast_to(jnp.sum(flags, axis=0, keepdims=True), (SUBLANES, LANES))
+    count = jnp.sum(flags, axis=0, keepdims=True)
+    count = jnp.where(free[:1], count, 0.0)
+    count = jnp.max(count, axis=1, keepdims=True)
+    count = jnp.broadcast_to(count, (SUBLANES, LANES))
     per_one = 1.0 / count
     per_pair = per_one / (count - 1.0)
     skill_weight, spread_weight = [], []
@@ -207,9 +219,6 @@
         row = jnp.where(lane == u, one, row)
     partials[pl.ds(mine, 1), :] = row * weight
 
-    for send in sends:
-        send.wait_send()
-
     def share_with(far):
         return pltpu.make_async_remote_copy(
             src_ref=partials.at[pl.ds(mine, 1)],
@@ -237,12 +246,14 @@
         piece = blocks[at // SUBLANES][at % SUBLANES : at % SUBLANES + 1, first : first + wide]
         field_ref[u // leads, u % leads, :, pl.ds(low, wide)] = piece
 
+    for send in sends:
+        send.wait_send()
+    for far in range(total):
+        pl.when(far != mine)(lambda far=far: share_with(far).wait_send())
     for far in range(total):
         pl.when(far != mine)(lambda far=far: share_from(far).wait_recv())
     summed = jnp.sum(partials[...], axis=0, keepdims=True)
     table_ref[...] = summed[:, :units] / (nz * rows * GRID_LON)
-    for far in range(total):
-        pl.when(far != mine)(lambda far=far: share_with(far).wait_send())
 
 
 def write_out(field_ref, table_ref, field_out, table_out, sem):
@@ -261,7 +272,8 @@
     assert rows == n and rows % SUBLANES == 0
     units = variables * leads
     packing = Packing(units, lon)
-    pitch = round_up(held * packing.lines + held, SUBLANES)
+    assert packing.tails and packing.used < LANES
+    pitch = round_up(held * packing.lines, SUBLANES)
     stride = round_up(packing.lines, SUBLANES)
     total = n * nz
     field, table = pl.pallas_call(

time: 17.8 us -> 17.5 us (0.983)
  Pallas kernels: 16.3 us -> 16.1 us
    pallas_call x1, Pallas kernels: 15.7 us -> 15.5 us  [on_device(): pl.pallas_call(functools.partial(kernel, n, nz), out_shape=(pltpu.VMEM((v...]
where the time goes in v4:
time: 17.5 us; the launch traced here: 17.4 us
  Pallas kernels  16.1 us (92%)
  between operations  1.28 us (7%)
    pallas_call x1, Pallas kernels, on_device(): pl.pallas_call(functools.partial(kernel, n, nz), out_shape=(pltpu.VMEM((v...  15.5 us
    pallas_call x1, Pallas kernels, on_device(): pl.pallas_call(write_out, out_shape=(jax.ShapeDtypeStruct(field.shape, jn...  0.63 us

profile of v4, /device:TPU:0, one launch (start us, length us, event | category | flops | bytes accessed | tf_op | source)
XLA Modules:
  0.0 17.4 jit_solution(15030007093115850378)
XLA Ops:
  1.3 15.5 %fair_crps.1 = (f32[3,1,1,1440]{3,2,1,0:T(1,128)S(1)}, f32[1,3]{1,0:T(1,128)S(1)}) custom-call(f32[2,3,1,8,1440]{4,3,2,1,0:T(8,128)} %ens_ref.1, f32[3,1,8,1440]{3,2,1,0:T(8,128)} %obs_ref.1, s32[2]{0:T(128)} %mask_ref.1, s32[1]{0:T(128)S(6)} %copy.6.band_ref), custom_call_target="tpu_custom_call" | custom-call | tf_op jit(solution)/shard_map/fair_crps/pallas_call | solution.py:279
  16.8 0.6 %write_out.1 = (f32[3,1,1,1440]{3,2,1,0:T(1,128)}, f32[1,3]{1,0:T(1,128)}) custom-call(f32[3,1,1,1440]{3,2,1,0:T(1,128)S(1)} %get-tuple-element.6.field_ref, f32[1,3]{1,0:T(1,128)S(1)} %get-tuple-element.7.table_ref), custom_call_target="tpu_custom_call" | custom-call | tf_op jit(solution)/shard_map/write_out/pallas_call | solution.py:310
